TPU v7x, 32 devices: a whole 2x2x4 slice. The times are simulated.
32 devices in a mesh: gz: 4 (over y, x), gy: 8 (over z, core).
Axes of the slice: x: 2, y: 2, z: 4, core: 2. Of those that a mesh axis runs over, the one named last changes fastest.
Arguments:
- grid_grad: float32 [64, 128, 512], P('gz', 'gy'), may hold values from -6 to 6
- cells: int32 [3, 65536], P(None, ('gz', 'gy')), may hold values from 0 to 511, as said below
- offsets: int32 [3, 65536], P(None, ('gz', 'gy')), may hold values from 0 to 1023
- owners: int32 [65536, 1], P(('gz', 'gy')), may hold values from 0 to 31; in each aligned block of 2048 rows (0 to 2047, 2048 to 4095, ...) at most 128 rows name the same one
- slots: int32 [65536], P(('gz', 'gy')), may hold values from 0 to 2047
Outputs:
- pos_grad: float32 [3, 65536], P(None, ('gz', 'gy'))
Inputs may be any that keep to these rules, and one draw needn't show every extreme that they name: `cells`: the row's cell lies in the mesh block of the device that holds the row: along z in [gz * 16, gz * 16 + 16), along y in [gy * 16, gy * 16 + 16), where gz, gy are that device's indices. `owners`: owners are linear device indices gz * 8 + gy. Among the rows of one device, no owner is named by more than 128 rows; some owner is named by exactly 128.
All inputs are finite; a program needn't handle non-finite values.
Results may differ from a plain program's by a relative error of at most 0.0003.
Values sent between devices are 32-bit elements; how exact they have to be, the bound alone decides.
A program may use at most 64 MiB of HBM per device.

v0:
```python
import jax
import jax.numpy as jnp
from jax import lax
from jax.sharding import PartitionSpec as P


def from_behind(block, axis, distance):
    devices = range(lax.axis_size(axis))
    route = [((i - distance) % len(devices), i) for i in devices]
    return lax.ppermute(block, axis, route)


def two_weights(index, frac, length):
    places = lax.broadcasted_iota(jnp.int32, (index.shape[0], length), 1)
    lower = (places == index[:, None]).astype(jnp.float32)
    upper = (places == ((index + 1) % length)[:, None]).astype(jnp.float32)
    weights = lower * (1.0 - frac)[:, None] + upper * frac[:, None]
    return (weights, upper - lower)


def body(grid_grad, cells, offsets, owners, slots):
    block_z, block_y, size_x = grid_grad.shape
    upper_z = from_behind(grid_grad[:1], "gz", -1)
    with_z = jnp.concatenate([grid_grad, upper_z], axis=0)
    upper_y = from_behind(with_z[:, :1], "gy", -1)
    extended = jnp.concatenate([with_z, upper_y], axis=1)
    ext_z = block_z + 1
    ext_y = block_y + 1
    plane = extended.reshape(ext_z * ext_y, size_x)
    local_z = cells[0] - lax.axis_index("gz") * block_z
    local_y = cells[1] - lax.axis_index("gy") * block_y
    fraction = (offsets.astype(jnp.float32) + 0.5) / 1024.0
    num_rows = cells.shape[1]
    rows_block = min(512, num_rows)
    num_blocks = num_rows // rows_block
    where_rows = jnp.stack([local_z, local_y, cells[2]])
    where_rows = where_rows.reshape(3, num_blocks, rows_block).transpose(1, 0, 2)
    frac_rows = fraction.reshape(3, num_blocks, rows_block).transpose(1, 0, 2)

    def read_block(carry, inputs):
        index, frac = inputs
        weight_x, diff_x = two_weights(index[2], frac[2], size_x)
        stacked = jnp.concatenate([weight_x, diff_x], axis=0)
        projected = lax.dot_general(
            stacked,
            plane,
            (((1,), (1,)), ((), ())),
            precision=lax.Precision.HIGHEST,
            preferred_element_type=jnp.float32,
        )
        projected = projected.reshape(2, index.shape[1], ext_z, ext_y)
        weight_z, diff_z = two_weights(index[0], frac[0], ext_z)
        weight_y, diff_y = two_weights(index[1], frac[1], ext_y)
        along_wy = jnp.sum(projected * weight_y[None, :, None, :], axis=3)
        along_dy = jnp.sum(projected[0] * diff_y[:, None, :], axis=2)
        grad_z = jnp.sum(along_wy[0] * diff_z, axis=1)
        grad_y = jnp.sum(along_dy * weight_z, axis=1)
        grad_x = jnp.sum(along_wy[1] * weight_z, axis=1)
        return (carry, jnp.stack([grad_z, grad_y, grad_x]))

    unused, read_out = lax.scan(read_block, 0, (where_rows, frac_rows))
    gradient = read_out.transpose(1, 0, 2).reshape(3, num_rows)
    count_z = lax.axis_size("gz")
    count_y = lax.axis_size("gy")
    devices_all = count_z * count_y
    capacity = 2 * num_rows // devices_all
    target = owners[:, 0]
    owner_hot = (
        target[:, None] == lax.broadcasted_iota(jnp.int32, (num_rows, devices_all), 1)
    ).astype(jnp.bfloat16)
    group = 128
    num_groups = num_rows // group
    grouped = owner_hot.reshape(num_groups, group, devices_all)
    lower_tri = (
        lax.broadcasted_iota(jnp.int32, (group, group), 0)
        > lax.broadcasted_iota(jnp.int32, (group, group), 1)
    ).astype(jnp.bfloat16)
    before = jnp.einsum("ij,gjd->gid", lower_tri, grouped, preferred_element_type=jnp.float32)
    group_counts = jnp.sum(grouped.astype(jnp.float32), axis=1)
    group_start = jnp.cumsum(group_counts, axis=0) - group_counts
    rank_float = jnp.sum(
        (before + group_start[:, None, :]) * grouped.astype(jnp.float32), axis=2
    ).reshape(num_rows)
    rank_int = rank_float.astype(jnp.int32)
    rank_hot = (
        rank_int[:, None] == lax.broadcasted_iota(jnp.int32, (num_rows, capacity), 1)
    ).astype(jnp.float32)
    values = jnp.concatenate([gradient, (slots + 1).astype(jnp.float32)[None]], axis=0)
    placed = jnp.einsum("cr,rk->ckr", values, rank_hot)
    send_all = jnp.einsum(
        "ckr,rd->ckd",
        placed,
        owner_hot.astype(jnp.float32),
        precision=lax.Precision.HIGHEST,
        preferred_element_type=jnp.float32,
    )
    send_grad = send_all[:3].reshape(3, capacity, count_z, count_y)
    slot_plus = send_all[3].astype(jnp.int32) - 1
    send_slot = jnp.where(slot_plus < 0, num_rows, slot_plus).reshape(1, capacity, count_z, count_y)
    recv_grad, recv_slot = (
        lax.all_to_all(
            lax.all_to_all(send_grad, "gz", split_axis=2, concat_axis=2, tiled=True),
            "gy",
            split_axis=3,
            concat_axis=3,
            tiled=True,
        ),
        lax.all_to_all(
            lax.all_to_all(send_slot, "gz", split_axis=2, concat_axis=2, tiled=True),
            "gy",
            split_axis=3,
            concat_axis=3,
            tiled=True,
        ),
    )
    recv_grad = recv_grad.reshape(3, -1)
    recv_slot = recv_slot.reshape(-1)
    received = recv_slot.shape[0]
    high_count = num_rows // 128
    slot_high = recv_slot // 128
    slot_low = recv_slot % 128
    high_hot = (
        slot_high[:, None] == lax.broadcasted_iota(jnp.int32, (received, high_count), 1)
    ).astype(jnp.float32)
    low_hot = (slot_low[:, None] == lax.broadcasted_iota(jnp.int32, (received, 128), 1)).astype(
        jnp.float32
    )
    spread = jnp.einsum("cm,mh->chm", recv_grad, high_hot)
    total = jnp.einsum(
        "chm,ml->chl",
        spread,
        low_hot,
        precision=lax.Precision.HIGHEST,
        preferred_element_type=jnp.float32,
    )
    return total.reshape(3, num_rows)


def solution(mesh):
    placed = (
        P("gz", "gy", None),
        P(None, ("gz", "gy")),
        P(None, ("gz", "gy")),
        P(("gz", "gy"), None),
        P(("gz", "gy")),
    )
    return jax.shard_map(
        body, mesh=mesh, in_specs=placed, out_specs=P(None, ("gz", "gy")), check_vma=False
    )
```

profile of v0, /device:TPU:0, one launch (start us, length us, event | category | flops | bytes accessed | tf_op | source)
XLA Modules:
  0.0 73.9 jit_solution(16124405531662332491)
XLA Ops:
  0.0 0.8 %slice.94 = f32[1,16,512]{2,1,0:T(8,128)S(1)} slice(f32[16,16,512]{2,1,0:T(8,128)} %param.7), slice={[0:1], [0:16], [0:512]} | slice | bytes 65536 | tf_op jit(solution)/shard_map/slice | solution.py:23
  0.8 3.9 %collective-permute-start = (f32[1,16,512]{2,1,0:T(8,128)S(1)}, f32[1,16,512]{2,1,0:T(8,128)S(1)}, u32[]{:S(2)}, u32[]{:S(2)}) collective-permute-start(f32[1,16,512]{2,1,0:T(8,128)S(1)} %slice.94), channel_id=1, source_target_pairs={{8,0},{16,8},{24,16},{0,24},{9,1},{17,9},{25,17},{1,25},{10,2},{18... | collective-permute-start | bytes 98312 | tf_op jit(solution)/shard_map/ppermute | solution.py:10
  4.8 0.8 %add_multiply_fusion = f32[3,2048]{1,0:T(4,128)S(1)} fusion(s32[3,2048]{1,0:T(4,128)} %param.9), kind=kLoop, calls=%fused_computation.80 | loop fusion | flops 18432 | bytes 49152 | tf_op jit(solution)/shard_map/div | solution.py:32
  5.5 0.7 add_convert_fusion
  6.2 0.8 %convert_reduce_fusion = f32[16,32]{1,0:T(8,128)S(1)} fusion(s32[16,128]{1,0:T(8,128)} %bitcast.128), kind=kLoop, calls=%fused_computation.64 | loop fusion | flops 261632 | bytes 10240 | tf_op jit(solution)/shard_map/reduce_sum | solution.py:79
  7.1 1.0 %fusion.20 = f32[16,128]{1,0:T(8,128)S(1)} fusion(f32[16,32]{1,0:T(8,128)S(1)} %sub.91, s32[16,128]{1,0:T(8,128)} %bitcast.129), kind=kOutput, calls=%fused_computation.54 | convolution fusion | flops 17250304 | bytes 18432 | tf_op jit(solution)/shard_map/ij,gjd->gid/dot_general | solution.py:78
  8.1 1.1 %fusion.25 = f32[2048,128]{0,1:T(8,128)} fusion(s32[2048]{0:T(1024)S(1)} %convert_bitcast_fusion), kind=kLoop, calls=%fused_computation.58 | loop fusion | flops 524288 | bytes 1056768 | tf_op jit(solution)/shard_map/convert
  9.4 2.8 %collective-permute-start.1 = (f32[17,1,512]{2,1,0:T(1,128)S(1)}, f32[17,1,512]{2,1,0:T(1,128)S(1)}, u32[]{:S(2)}, u32[]{:S(2)}) collective-permute-start(f32[17,1,512]{2,1,0:T(1,128)S(1)} %slice.101), channel_id=1, source_target_pairs={{1,0},{2,1},{3,2},{4,3},{5,4},{6,5},{7,6},{0,7},{9,8},{10,9},{11,1... | collective-permute-start | bytes 104456 | tf_op jit(solution)/shard_map/ppermute | solution.py:10
  12.2 1.6 %collective-permute-done.1 = f32[17,1,512]{2,1,0:T(1,128)S(1)} collective-permute-done((f32[17,1,512]{2,1,0:T(1,128)S(1)}, f32[17,1,512]{2,1,0:T(1,128)S(1)}, u32[]{:S(2)}, u32[]{:S(2)}) %collective-permute-start.1) | collective-permute-done | bytes 34848 | tf_op jit(solution)/shard_map/ppermute | solution.py:10
  14.0 18.9 %while.13 = (s32[]{:T(128)}, f32[4,3,512]{2,1,0:T(4,128)S(1)}, s32[4,3,512]{2,1,0:T(4,128)S(1)}, f32[4,3,512]{2,1,0:T(4,128)S(1)}, f32[289,512]{1,0:T(8,128)S(1)}, /*index=5*/s32[]{:T(128)}, s32[]{:T(128)}, s32[]{}, s32[]{}) while((s32[]{:T(128)}, f32[4,3,512]{2,1,0:T(4,128)S(1)}, s32[4,3,512]{2,1,0:T(4,128)S(1)}, ...), condition=%wide.region_9.10_spmd, body=%wide.region_3.9_spmd.sunk | while | flops 1821921792 | bytes 13062289 | solution.py:61
  14.1 0.4 select_add_fusion.5
  14.5 2.2 %fusion.51 = f32[1024,289]{0,1:T(8,128)S(1)} fusion(f32[289,512]{1,0:T(8,128)S(1)} %get-tuple-element.212, f32[512,512]{1,0:T(8,128)S(1)} %get-tuple-element.175, f32[512,512]{1,0:T(8,128)S(1)} %get-tuple-element.176), kind=kOutput, calls=%fused_computation.clone.1 | convolution fusion | flops 1818755072 | bytes 3872768 | tf_op jit(solution)/shard_map/while/body/eval_jaxpr/dot_general | solution.py:44
  16.9 0.2 multiply_reduce_fusion.6
  17.1 1.0 %reshape.346 = f32[2,512,17,17]{1,0,3,2:T(2,128)S(1)} reshape(f32[1024,289]{0,1:T(8,128)S(1)} %fusion.51) | data formatting | bytes 2367488 | tf_op jit(solution)/shard_map/while/body/eval_jaxpr/reshape | solution.py:51
  18.1 0.5 multiply_reduce_fusion.7
  18.8 0.4 select_add_fusion.5
  19.2 2.2 %fusion.51 = f32[1024,289]{0,1:T(8,128)S(1)} fusion(f32[289,512]{1,0:T(8,128)S(1)} %get-tuple-element.212, f32[512,512]{1,0:T(8,128)S(1)} %get-tuple-element.175, f32[512,512]{1,0:T(8,128)S(1)} %get-tuple-element.176), kind=kOutput, calls=%fused_computation.clone.1 | convolution fusion | flops 1818755072 | bytes 3872768 | tf_op jit(solution)/shard_map/while/body/eval_jaxpr/dot_general | solution.py:44
  21.6 0.2 multiply_reduce_fusion.6
  21.8 1.0 %reshape.346 = f32[2,512,17,17]{1,0,3,2:T(2,128)S(1)} reshape(f32[1024,289]{0,1:T(8,128)S(1)} %fusion.51) | data formatting | bytes 2367488 | tf_op jit(solution)/shard_map/while/body/eval_jaxpr/reshape | solution.py:51
  22.8 0.5 multiply_reduce_fusion.7
  23.5 0.4 select_add_fusion.5
  23.9 2.2 %fusion.51 = f32[1024,289]{0,1:T(8,128)S(1)} fusion(f32[289,512]{1,0:T(8,128)S(1)} %get-tuple-element.212, f32[512,512]{1,0:T(8,128)S(1)} %get-tuple-element.175, f32[512,512]{1,0:T(8,128)S(1)} %get-tuple-element.176), kind=kOutput, calls=%fused_computation.clone.1 | convolution fusion | flops 1818755072 | bytes 3872768 | tf_op jit(solution)/shard_map/while/body/eval_jaxpr/dot_general | solution.py:44
  26.4 0.2 multiply_reduce_fusion.6
  26.5 1.0 %reshape.346 = f32[2,512,17,17]{1,0,3,2:T(2,128)S(1)} reshape(f32[1024,289]{0,1:T(8,128)S(1)} %fusion.51) | data formatting | bytes 2367488 | tf_op jit(solution)/shard_map/while/body/eval_jaxpr/reshape | solution.py:51
  27.5 0.5 multiply_reduce_fusion.7
  28.3 0.4 select_add_fusion.5
  28.6 2.2 %fusion.51 = f32[1024,289]{0,1:T(8,128)S(1)} fusion(f32[289,512]{1,0:T(8,128)S(1)} %get-tuple-element.212, f32[512,512]{1,0:T(8,128)S(1)} %get-tuple-element.175, f32[512,512]{1,0:T(8,128)S(1)} %get-tuple-element.176), kind=kOutput, calls=%fused_computation.clone.1 | convolution fusion | flops 1818755072 | bytes 3872768 | tf_op jit(solution)/shard_map/while/body/eval_jaxpr/dot_general | solution.py:44
  31.1 0.2 multiply_reduce_fusion.6
  31.3 1.0 %reshape.346 = f32[2,512,17,17]{1,0,3,2:T(2,128)S(1)} reshape(f32[1024,289]{0,1:T(8,128)S(1)} %fusion.51) | data formatting | bytes 2367488 | tf_op jit(solution)/shard_map/while/body/eval_jaxpr/reshape | solution.py:51
  32.3 0.5 multiply_reduce_fusion.7
  33.0 3.5 %fusion.10 = f32[4,128,32]{1,2,0:T(8,128)S(1)} fusion(f32[2048,4]{0,1:T(4,128)S(1)} %maximum_bitcast_fusion.1, f32[2048,128]{0,1:T(8,128)} %fusion.25, s32[2048]{0:T(1024)S(1)} %bitcast.130), kind=kOutput, calls=%fused_computation.43 | convolution fusion | flops 403767296 | bytes 1155072 | tf_op jit(solution)/shard_map/ckr,rd->ckd/dot_general | solution.py:90
  36.5 0.6 compare_select_fusion
  37.1 3.3 %all-to-all-start = ((s32[1,128,4,8]{1,3,0,2:T(8,128)}), s32[1,128,4,8]{1,3,0,2:T(8,128)S(1)}, u32[]{:S(2)}, u32[]{:S(2)}) async-start(s32[1,128,4,8]{1,3,0,2:T(8,128)} %compare_select_fusion), calls=%async_computation | async-start | bytes 32768 | tf_op jit(solution)/shard_map/all_to_all | solution.py:109
  40.3 0.6 copy.14
  41.0 4.0 %all-to-all-done = s32[1,128,4,8]{1,3,0,2:T(8,128)S(1)} async-done(((s32[1,128,4,8]{1,3,0,2:T(8,128)}), s32[1,128,4,8]{1,3,0,2:T(8,128)S(1)}, u32[]{:S(2)}, u32[]{:S(2)}) %all-to-all-start) | async-done | bytes 16416 | tf_op jit(solution)/shard_map/all_to_all | solution.py:109
  45.0 3.3 %all-to-all-start.2 = ((f32[3,128,4,8]{1,3,0,2:T(8,128)}), f32[3,128,4,8]{1,3,0,2:T(8,128)S(1)}, u32[]{:S(2)}, u32[]{:S(2)}) async-start(f32[3,128,4,8]{1,3,0,2:T(8,128)} %copy.14), calls=%async_computation.2 | async-start | bytes 98304 | tf_op jit(solution)/shard_map/all_to_all | solution.py:102
  48.3 0.6 copy.12
  48.9 4.2 %all-to-all-done.2 = f32[3,128,4,8]{1,3,0,2:T(8,128)S(1)} async-done(((f32[3,128,4,8]{1,3,0,2:T(8,128)}), f32[3,128,4,8]{1,3,0,2:T(8,128)S(1)}, u32[]{:S(2)}, u32[]{:S(2)}) %all-to-all-start.2) | async-done | bytes 49184 | tf_op jit(solution)/shard_map/all_to_all | solution.py:102
  53.1 3.3 %all-to-all-start.1 = ((s32[1,128,4,8]{1,2,0,3:T(4,128)}), s32[1,128,4,8]{1,2,0,3:T(4,128)S(1)}, u32[]{:S(2)}, u32[]{:S(2)}) async-start(s32[1,128,4,8]{1,2,0,3:T(4,128)} %copy.12), calls=%async_computation.1 | async-start | bytes 32768 | tf_op jit(solution)/shard_map/all_to_all | solution.py:108
  56.4 0.6 copy.15
  57.0 5.0 %all-to-all-done.1 = s32[1,128,4,8]{1,2,0,3:T(4,128)S(1)} async-done(((s32[1,128,4,8]{1,2,0,3:T(4,128)}), s32[1,128,4,8]{1,2,0,3:T(4,128)S(1)}, u32[]{:S(2)}, u32[]{:S(2)}) %all-to-all-start.1) | async-done | bytes 16416 | tf_op jit(solution)/shard_map/all_to_all | solution.py:108
  62.0 3.3 %all-to-all-start.3 = ((f32[3,128,4,8]{1,2,0,3:T(4,128)}), f32[3,128,4,8]{1,2,0,3:T(4,128)S(1)}, u32[]{:S(2)}, u32[]{:S(2)}) async-start(f32[3,128,4,8]{1,2,0,3:T(4,128)} %copy.15), calls=%async_computation.3 | async-start | bytes 98304 | tf_op jit(solution)/shard_map/all_to_all | solution.py:101
  65.5 0.2 reshape.337
  65.8 5.3 %all-to-all-done.3 = f32[3,128,4,8]{1,2,0,3:T(4,128)S(1)} async-done(((f32[3,128,4,8]{1,2,0,3:T(4,128)}), f32[3,128,4,8]{1,2,0,3:T(4,128)S(1)}, u32[]{:S(2)}, u32[]{:S(2)}) %all-to-all-start.3) | async-done | bytes 49184 | tf_op jit(solution)/shard_map/all_to_all | solution.py:101
  71.1 0.3 copy.16
  71.4 0.8 %reshape.339 = f32[3,4096]{1,0:T(4,128)S(1)} reshape(f32[3,128,4,8]{3,2,1,0:T(4,128)S(1)} %copy.16) | data formatting | bytes 98304 | tf_op jit(solution)/shard_map/reshape | solution.py:116
  72.2 1.0 %fusion.21 = f32[1,3,16,128]{3,2,1,0:T(8,128)S(1)} fusion(s32[4096]{0:T(1024)S(1)} %get-tuple-element.124, f32[4096,3]{0,1:T(4,128)S(1)} %bitcast.122, f32[4096,16]{0,1:T(8,128)S(1)} %fusion.33), kind=kOutput, calls=%fused_computation.55 | convolution fusion | flops 302710784 | bytes 352256 | tf_op jit(solution)/shard_map/chm,ml->chl/dot_general | solution.py:129
  73.2 0.6 copy.27
  (75 shorter events, 2.0 us)
Async XLA Ops:
  0.0 9.3 %copy-start = (f32[16,16,512]{2,1,0:T(8,128)S(1)}, f32[16,16,512]{2,1,0:T(8,128)}, u32[]{:S(2)}) copy-start(f32[16,16,512]{2,1,0:T(8,128)} %param.7) | copy-start | bytes 1572868
  0.0 9.2 %copy-start.1 = (s32[3,2048]{1,0:T(4,128)S(1)}, s32[3,2048]{1,0:T(4,128)}, u32[]{:S(2)}) copy-start(s32[3,2048]{1,0:T(4,128)} %param.8) | copy-start | bytes 73732
  0.8 8.5 %collective-permute-start = (f32[1,16,512]{2,1,0:T(8,128)S(1)}, f32[1,16,512]{2,1,0:T(8,128)S(1)}, u32[]{:S(2)}, u32[]{:S(2)}) collective-permute-start(f32[1,16,512]{2,1,0:T(8,128)S(1)} %slice.94), channel_id=1, source_target_pairs={{8,0},{16,8},{24,16},{0,24},{9,1},{17,9},{25,17},{1,25},{10,2},{18... | collective-permute-start | bytes 98312 | tf_op jit(solution)/shard_map/ppermute | solution.py:10
  9.4 4.4 %collective-permute-start.1 = (f32[17,1,512]{2,1,0:T(1,128)S(1)}, f32[17,1,512]{2,1,0:T(1,128)S(1)}, u32[]{:S(2)}, u32[]{:S(2)}) collective-permute-start(f32[17,1,512]{2,1,0:T(1,128)S(1)} %slice.101), channel_id=1, source_target_pairs={{1,0},{2,1},{3,2},{4,3},{5,4},{6,5},{7,6},{0,7},{9,8},{10,9},{11,1... | collective-permute-start | bytes 104456 | tf_op jit(solution)/shard_map/ppermute | solution.py:10
  14.0 18.9 %copy-start.2 = (s32[2048,1]{0,1:T(1,128)S(1)}, s32[2048,1]{0,1:T(1,128)}, u32[]{:S(2)}) copy-start(s32[2048,1]{0,1:T(1,128)} %param.10) | copy-start | bytes 24580
  37.1 7.9 %all-to-all-start = ((s32[1,128,4,8]{1,3,0,2:T(8,128)}), s32[1,128,4,8]{1,3,0,2:T(8,128)S(1)}, u32[]{:S(2)}, u32[]{:S(2)}) async-start(s32[1,128,4,8]{1,3,0,2:T(8,128)} %compare_select_fusion), calls=%async_computation | async-start | bytes 32768 | tf_op jit(solution)/shard_map/all_to_all | solution.py:109
  45.0 8.0 %all-to-all-start.2 = ((f32[3,128,4,8]{1,3,0,2:T(8,128)}), f32[3,128,4,8]{1,3,0,2:T(8,128)S(1)}, u32[]{:S(2)}, u32[]{:S(2)}) async-start(f32[3,128,4,8]{1,3,0,2:T(8,128)} %copy.14), calls=%async_computation.2 | async-start | bytes 98304 | tf_op jit(solution)/shard_map/all_to_all | solution.py:102
  53.1 8.9 %all-to-all-start.1 = ((s32[1,128,4,8]{1,2,0,3:T(4,128)}), s32[1,128,4,8]{1,2,0,3:T(4,128)S(1)}, u32[]{:S(2)}, u32[]{:S(2)}) async-start(s32[1,128,4,8]{1,2,0,3:T(4,128)} %copy.12), calls=%async_computation.1 | async-start | bytes 32768 | tf_op jit(solution)/shard_map/all_to_all | solution.py:108
  62.0 9.1 %all-to-all-start.3 = ((f32[3,128,4,8]{1,2,0,3:T(4,128)}), f32[3,128,4,8]{1,2,0,3:T(4,128)S(1)}, u32[]{:S(2)}, u32[]{:S(2)}) async-start(f32[3,128,4,8]{1,2,0,3:T(4,128)} %copy.15), calls=%async_computation.3 | async-start | bytes 98304 | tf_op jit(solution)/shard_map/all_to_all | solution.py:101
where the time goes:
time: 74.5 us; the launch traced here: 73.9 us
  waiting for transfers between devices  20 us (27%)
  starting transfers between devices  19.9 us (27%)
  matrix products  14.4 us (19%)
  local copies, waits for them, and re-layouts  9.89 us (13%)
  other arithmetic  8.8 us (12%)
    dot_general x4, matrix products, read_block(): lax.dot_general(stacked, plane, (((1,), (1,)), ((), ())), precision=lax.P...  8.93 us
    ppermute x2, starting transfers between devices, from_behind(): return lax.ppermute(block, axis, route)  6.74 us
    all_to_all x1, waiting for transfers between devices, body(): lax.all_to_all(lax.all_to_all(send_grad, 'gz', split_axis=2, concat_axis=...  5.31 us
    all_to_all x1, waiting for transfers between devices, body(): lax.all_to_all(lax.all_to_all(send_slot, 'gz', split_axis=2, concat_axis=...  4.95 us
    all_to_all x1, waiting for transfers between devices, body(): lax.all_to_all(send_grad, 'gz', split_axis=2, concat_axis=2, tiled=True)  4.16 us
    all_to_all x1, waiting for transfers between devices, body(): lax.all_to_all(send_slot, 'gz', split_axis=2, concat_axis=2, tiled=True)  4.04 us
    reshape x4, local copies, waits for them, and re-layouts, read_block(): projected = projected.reshape(2, index.shape[1], ext_z, ext_y)  4.02 us
    dot_general x1, matrix products, body(): jnp.einsum('ckr,rd->ckd', placed, owner_hot.astype(jnp.float32), precisio...  3.49 us
  transfers between devices with their start and end apart: 6, of which 5 were waited for; matrix products, arithmetic and copies ran while one was open for 9% of the time, Pallas kernels for 0%

commit v1 on v0

v1 whole, which is shorter than its diff:
```python
import functools

import jax
import jax.numpy as jnp
from jax import lax
from jax.experimental import pallas as pl
from jax.experimental.pallas import tpu as pltpu
from jax.sharding import PartitionSpec as P

MESH = pl.DeviceIdType.MESH
BF = jnp.bfloat16
F32 = jnp.float32
LANES = 128


def iota(shape, axis):
    return lax.broadcasted_iota(jnp.int32, shape, axis)


def hot(mask):
    return jnp.where(mask, 1.0, 0.0).astype(BF)


def split(value):
    high = value.astype(BF)
    low = (value - high.astype(F32)).astype(BF)
    return high, low


def dot_nn(a, b):
    return lax.dot_general(a, b, (((1,), (0,)), ((), ())), preferred_element_type=F32)


def dot_nt(a, b):
    return lax.dot_general(a, b, (((1,), (1,)), ((), ())), preferred_element_type=F32)


def with_diff(rows):
    size_x = rows.shape[1]
    diff = pltpu.roll(rows, size_x - 1, 1) - rows
    return jnp.concatenate([*split(rows), *split(diff)], axis=0)


def over(count, step, carry):
    if count == 1:
        return step(0, carry)
    return lax.fori_loop(0, count, step, carry)


def kernel(
    grid_ref, cells, offsets, owners, slots, out,
    grid_v, row_s, corner_s, halo_z, halo_y, halo_c, mesh_s, hot_s, acc_s, rank_s, vals_s,
    send_s, recv_s, grid_sem, halo_send, halo_recv, all_send, all_recv,
):
    count_z, count_y = lax.axis_size("gz"), lax.axis_size("gy")
    devices = count_z * count_y
    gz, gy = lax.axis_index("gz"), lax.axis_index("gy")
    me = gz * count_y + gy
    size_z, size_y, size_x = grid_ref.shape
    rows = cells.shape[1]
    chunk = min(256, rows)
    chunks = rows // chunk
    group = min(32, devices)
    groups = devices // group
    slab = size_z * size_y

    load = pltpu.make_async_copy(grid_ref, grid_v, grid_sem)
    load.start()
    barrier = pltpu.get_barrier_semaphore()

    def coords(shift):
        other = lax.rem(me + shift, devices)
        return (other // count_y, lax.rem(other, count_y))

    def greet(shift, carry):
        pl.semaphore_signal(barrier, inc=1, device_id=coords(shift), device_id_type=MESH)
        return carry

    lax.fori_loop(1, devices, greet, 0)

    owner = owners[...]
    before = hot(iota((chunk, chunk), 0) < iota((chunk, chunk), 1))

    def rank_group(g, ranks):
        mine = jnp.where(iota((group, rows), 0) + g * group == owner, 1.0, 0.0)
        pieces = [mine[:, c * chunk:(c + 1) * chunk] for c in range(chunks)]
        inside = dot_nn(jnp.concatenate(pieces, axis=0).astype(BF), before)
        start = jnp.zeros((group, 1), F32)
        found = []
        for c in range(chunks):
            where = inside[c * group:(c + 1) * group] + start
            found.append(jnp.sum(pieces[c] * where, axis=0, keepdims=True))
            start = start + jnp.sum(pieces[c], axis=1, keepdims=True)
        return ranks + jnp.concatenate(found, axis=1)

    ranks = over(groups, rank_group, jnp.zeros((1, rows), F32))
    rank_s[...] = hot(iota((LANES, rows), 0) == ranks.astype(jnp.int32))

    load.wait()
    row_s[...] = grid_v[:, 0, :]
    corner_s[...] = grid_v[0, 0:1, :]
    mesh_s[...] = with_diff(grid_v[...].reshape(slab, size_x))

    pl.semaphore_wait(barrier, devices - 1)
    below_z = lax.rem(gz + count_z - 1, count_z)
    below_y = lax.rem(gy + count_y - 1, count_y)
    halos = []
    for i, (source, target, device) in enumerate((
        (grid_ref.at[0], halo_z, (below_z, gy)),
        (row_s, halo_y, (gz, below_y)),
        (corner_s, halo_c, (below_z, below_y)),
    )):
        halos.append(pltpu.make_async_remote_copy(
            src_ref=source, dst_ref=target, send_sem=halo_send.at[i], recv_sem=halo_recv.at[i],
            device_id=device, device_id_type=MESH,
        ))
        halos[-1].start()

    def place(j):
        span = pl.ds(pl.multiple_of(j * chunk, chunk), chunk)
        cell = cells[:, span]
        frac = (offsets[:, span].astype(F32) + 0.5) / 1024.0
        return (span, cell[0:1] - gz * size_z, cell[1:2] - gy * size_y, cell[2:3],
                frac[0:1], frac[1:2], frac[2:3])

    def main_chunk(j, carry):
        span, cz, cy, cx, fz, fy, fx = place(j)
        onehot = hot(iota((size_x, chunk), 0) == cx)
        hot_s[:, span] = onehot
        prod = dot_nn(mesh_s[...], onehot)
        shape = (size_y, chunk)
        cz, fz = jnp.broadcast_to(cz, shape), jnp.broadcast_to(fz, shape)
        gz0 = 1.0 - fz
        total = [jnp.zeros(shape, F32) for _ in range(4)]
        for z in range(size_z):
            lower, upper = cz == z, cz == z - 1
            weight = jnp.where(lower, gz0, jnp.where(upper, fz, 0.0))
            diff = jnp.where(lower, -1.0, jnp.where(upper, 1.0, 0.0))
            at = [prod[q * slab + z * size_y:q * slab + (z + 1) * size_y] for q in range(4)]
            value, slope = at[0] + at[1], at[2] + at[3]
            total[0] += weight * value
            total[1] += diff * value
            total[2] += weight * slope
            total[3] += diff * slope
        for q in range(4):
            acc_s[q, :, span] = total[q]
        return carry

    lax.fori_loop(0, chunks, main_chunk, 0)

    for copy in halos:
        copy.wait()
    ghost = jnp.concatenate(
        [halo_z[...], halo_y[...], jnp.broadcast_to(halo_c[...], (8, size_x))], axis=0)
    ghost = with_diff(ghost)
    part = size_y + size_z + 8

    def halo_chunk(j, carry):
        span, cz, cy, cx, fz, fy, fx = place(j)
        prod = dot_nn(ghost, hot_s[:, span])
        value = prod[:part] + prod[part:2 * part]
        slope = prod[2 * part:3 * part] + prod[3 * part:]
        top_z, top_y = cz == size_z - 1, cy == size_y - 1
        wz_top, dz_top = jnp.where(top_z, fz, 0.0), jnp.where(top_z, 1.0, 0.0)
        wy_top, dy_top = jnp.where(top_y, fy, 0.0), jnp.where(top_y, 1.0, 0.0)
        a_w = acc_s[0, :, span] + wz_top * value[:size_y]
        a_d = acc_s[1, :, span] + dz_top * value[:size_y]
        b_w = acc_s[2, :, span] + wz_top * slope[:size_y]
        b_d = acc_s[3, :, span] + dz_top * slope[:size_y]
        place_y = iota((size_y, chunk), 0)
        lower, upper = place_y == cy, place_y == cy + 1
        w_y = jnp.where(lower, 1.0 - fy, jnp.where(upper, fy, 0.0))
        d_y = jnp.where(lower, -1.0, jnp.where(upper, 1.0, 0.0))
        grad_z = jnp.sum((a_d + fx * b_d) * w_y, axis=0, keepdims=True)
        grad_y = jnp.sum((a_w + fx * b_w) * d_y, axis=0, keepdims=True)
        grad_x = jnp.sum(b_w * w_y, axis=0, keepdims=True)
        place_z = iota((size_z, chunk), 0)
        lower, upper = place_z == cz, place_z == cz + 1
        w_z = jnp.where(lower, 1.0 - fz, jnp.where(upper, fz, 0.0))
        d_z = jnp.where(lower, -1.0, jnp.where(upper, 1.0, 0.0))
        side = slice(size_y, size_y + size_z)
        corner = slice(size_y + size_z, size_y + size_z + 1)
        read = value[side] + fx * slope[side]
        read_c = value[corner] + fx * slope[corner]
        h_w = jnp.sum(read * w_z, axis=0, keepdims=True) + read_c * wz_top
        h_d = jnp.sum(read * d_z, axis=0, keepdims=True) + read_c * dz_top
        h_x = jnp.sum(slope[side] * w_z, axis=0, keepdims=True) + slope[corner] * wz_top
        record = (slots[:, span] + 1).astype(F32)
        vals_s[:, span] = jnp.concatenate(
            [grad_z + wy_top * h_d, grad_y + dy_top * h_w, grad_x + wy_top * h_x, record] * 2, axis=0)
        return carry

    lax.fori_loop(0, chunks, halo_chunk, 0)

    def pack_group(g, carry):
        wide = 4 * group
        whose = lax.shift_right_logical(iota((wide, rows), 0), 2) + g * group
        values = jnp.concatenate([vals_s[...]] * (wide // 8), axis=0)
        high, low = split(jnp.where(whose == owner, values, 0.0))
        packed = dot_nt(high, rank_s[...]) + dot_nt(low, rank_s[...])
        for d in range(group):
            send_s[g * group + d] = packed[4 * d:4 * d + 4]
        return carry

    over(groups, pack_group, 0)

    def exchange(source, target, device):
        return pltpu.make_async_remote_copy(
            src_ref=source, dst_ref=target, send_sem=all_send, recv_sem=all_recv,
            device_id=device, device_id_type=MESH,
        )

    def post(shift, carry):
        other = lax.rem(me + shift, devices)
        exchange(send_s.at[other], recv_s.at[me], coords(shift)).start()
        return carry

    lax.fori_loop(1, devices, post, 0)
    recv_s[me] = send_s[me]
    others = pl.ds(0, devices - 1)
    exchange(send_s.at[others], recv_s.at[others], coords(1)).wait()

    highs = rows // LANES

    def add_group(g, total):
        block = jnp.concatenate([recv_s[g * group + d] for d in range(group)], axis=1)
        record = block[3:4].astype(jnp.int32) - 1
        high_at = lax.shift_right_arithmetic(record, 7)
        low_at = lax.bitwise_and(record, LANES - 1)
        width = block.shape[1]
        low_hot = hot(iota((LANES, width), 0) == low_at)
        values = jnp.concatenate([block] * highs, axis=0)
        which = lax.shift_right_logical(iota((4 * highs, width), 0), 2)
        both = jnp.concatenate(split(jnp.where(which == high_at, values, 0.0)), axis=0)
        added = dot_nt(both, low_hot)
        return total + added[:4 * highs] + added[4 * highs:]

    total = over(groups, add_group, jnp.zeros((4 * highs, LANES), F32))
    for h in range(highs):
        out[:, h * LANES:(h + 1) * LANES] = total[4 * h:4 * h + 3]


def body(grid_grad, cells, offsets, owners, slots):
    size_z, size_y, size_x = grid_grad.shape
    rows = cells.shape[1]
    devices = lax.axis_size("gz") * lax.axis_size("gy")
    vmem = pl.BlockSpec(memory_space=pltpu.VMEM)
    part = size_y + size_z + 8
    return pl.pallas_call(
        kernel,
        out_shape=jax.ShapeDtypeStruct((3, rows), F32),
        in_specs=[pl.BlockSpec(memory_space=pl.ANY), vmem, vmem, vmem, vmem],
        out_specs=vmem,
        scratch_shapes=[
            pltpu.VMEM((size_z, size_y, size_x), F32),
            pltpu.VMEM((size_z, size_x), F32),
            pltpu.VMEM((1, size_x), F32),
            pltpu.VMEM((size_y, size_x), F32),
            pltpu.VMEM((size_z, size_x), F32),
            pltpu.VMEM((1, size_x), F32),
            pltpu.VMEM((4 * size_z * size_y, size_x), BF),
            pltpu.VMEM((size_x, rows), BF),
            pltpu.VMEM((4, size_y, rows), F32),
            pltpu.VMEM((LANES, rows), BF),
            pltpu.VMEM((8, rows), F32),
            pltpu.VMEM((devices, 4, LANES), F32),
            pltpu.VMEM((devices, 4, LANES), F32),
            pltpu.SemaphoreType.DMA,
            pltpu.SemaphoreType.DMA((3,)),
            pltpu.SemaphoreType.DMA((3,)),
            pltpu.SemaphoreType.DMA,
            pltpu.SemaphoreType.DMA,
        ],
        compiler_params=pltpu.CompilerParams(collective_id=0, has_side_effects=True),
        name="cic",
    )(grid_grad, cells, offsets, owners.reshape(1, rows), slots.reshape(1, rows))


def solution(mesh):
    placed = (
        P("gz", "gy", None),
        P(None, ("gz", "gy")),
        P(None, ("gz", "gy")),
        P(("gz", "gy"), None),
        P(("gz", "gy")),
    )
    return jax.shard_map(
        body, mesh=mesh, in_specs=placed, out_specs=P(None, ("gz", "gy")), check_vma=False
    )
```

time: 74.5 us -> 21.8 us (0.29)
  Pallas kernels: 0 us -> 20.1 us
  waiting for transfers between devices: 20 us -> 0 us
  starting transfers between devices: 19.9 us -> 0 us
  matrix products: 14.4 us -> 0 us
  other arithmetic: 8.8 us -> 0 us
  local copies, waits for them, and re-layouts: 9.89 us -> 1.38 us
    pallas_call x0 -> x1, Pallas kernels: none -> 20.1 us  [body(): pl.pallas_call(kernel, out_shape=jax.ShapeDtypeStruct((3, rows), F32), in...]
    all_to_all x4 -> x0, waiting for transfers between devices: 18.5 us -> none  [the longest x1 5.31 us: body(): lax.all_to_all(lax.all_to_all(send_grad, 'gz', split_axis=2, concat_axis=...]
    dot_general x7 -> x0, matrix products: 14.4 us -> none  [the longest x4 8.93 us: read_block(): lax.dot_general(stacked, plane, (((1,), (1,)), ((), ())), precision=lax.P...]
    all_to_all x4 -> x0, starting transfers between devices: 13.2 us -> none  [the longest x1 3.35 us: body(): lax.all_to_all(lax.all_to_all(send_grad, 'gz', split_axis=2, concat_axis=...]
    ppermute x2 -> x0, starting transfers between devices: 6.74 us -> none  [from_behind(): return lax.ppermute(block, axis, route)]
    reshape x9 -> x0, local copies, waits for them, and re-layouts: 5.78 us -> none  [the longest x4 4.02 us: read_block(): projected = projected.reshape(2, index.shape[1], ext_z, ext_y)]
    reduce_sum x13 -> x0, other arithmetic: 3.6 us -> none  [the longest x4 1.9 us: read_block(): along_wy = jnp.sum(projected * weight_y[None, :, None, :], axis=3)]
    all_to_all x4 -> x0, local copies, waits for them, and re-layouts: 1.71 us -> none  [the longest x1 0.63 us: body(): lax.all_to_all(send_grad, 'gz', split_axis=2, concat_axis=2, tiled=True)]
  transfers between devices with their start and end apart: 6 -> 0, of which waited for: 5 -> 0; matrix products, arithmetic and copies ran while one was open for 9% -> 0% of each run, Pallas kernels for 0% -> 0%
where the time goes in v1:
time: 21.8 us; the launch traced here: 21.5 us
  Pallas kernels  20.1 us (92%)
  local copies, waits for them, and re-layouts  1.38 us (6%)
    pallas_call x1, Pallas kernels, body(): pl.pallas_call(kernel, out_shape=jax.ShapeDtypeStruct((3, rows), F32), in...  20.1 us
    unnamed x1, local copies, waits for them, and re-layouts  1.38 us

profile of v1, /device:TPU:0, one launch (start us, length us, event | category | flops | bytes accessed | tf_op | source)
XLA Modules:
  0.0 21.5 jit_solution(12269376857319103305)
XLA Ops:
  0.0 20.1 %cic.1 = f32[3,2048]{1,0:T(4,128)} custom-call(f32[16,16,512]{2,1,0:T(8,128)} %grid_ref.1, s32[3,2048]{1,0:T(4,128)} %cells.1, s32[3,2048]{1,0:T(4,128)} %offsets.1, s32[1,2048]{1,0:T(1,128)} %bitcast.2, s32[1,2048]{1,0:T(1,128)} %bitcast.3), custom_call_target="tpu_custom_call" | custom-call | tf_op jit(solution)/shard_map/cic/pallas_call | solution.py:249
  20.1 1.4 %copy.7 = f32[3,2048]{1,0:T(4,128)} copy(f32[3,2048]{1,0:T(4,128)} %cic.1) | data formatting | bytes 49152

commit v2 on v1

--- a/solution.py
+++ b/solution.py
@@ -1,5 +1,3 @@
-import functools
-
 import jax
 import jax.numpy as jnp
 from jax import lax
@@ -48,9 +46,9 @@
 
 
 def kernel(
-    grid_ref, cells, offsets, owners, slots, out,
-    grid_v, row_s, corner_s, halo_z, halo_y, halo_c, mesh_s, hot_s, acc_s, rank_s, vals_s,
-    send_s, recv_s, grid_sem, halo_send, halo_recv, all_send, all_recv,
+    grid_ref, cells_ref, offsets_ref, owners_ref, slots_ref, out,
+    cells, offsets, owners, slots, grid_v, row_s, corner_s, halo_z, halo_y, halo_c, mesh_s, hot_s, acc_s, rank_s, vals_s,
+    send_s, recv_s, load_sem, halo_send, halo_recv, all_send, all_recv,
 ):
     count_z, count_y = lax.axis_size("gz"), lax.axis_size("gy")
     devices = count_z * count_y
@@ -64,20 +62,37 @@
     groups = devices // group
     slab = size_z * size_y
 
-    load = pltpu.make_async_copy(grid_ref, grid_v, grid_sem)
-    load.start()
+    loads = []
+    for i, (source, target) in enumerate((
+        (owners_ref, owners), (grid_ref, grid_v), (cells_ref, cells),
+        (offsets_ref, offsets), (slots_ref, slots),
+    )):
+        loads.append(pltpu.make_async_copy(source, target, load_sem.at[i]))
+        loads[-1].start()
     barrier = pltpu.get_barrier_semaphore()
 
-    def coords(shift):
-        other = lax.rem(me + shift, devices)
-        return (other // count_y, lax.rem(other, count_y))
-
-    def greet(shift, carry):
-        pl.semaphore_signal(barrier, inc=1, device_id=coords(shift), device_id_type=MESH)
-        return carry
-
-    lax.fori_loop(1, devices, greet, 0)
-
+    def each_other(act):
+        few = devices <= 64
+
+        def along_y(to_z, first):
+            def step(shift, carry):
+                act(to_z, lax.rem(gy + shift, count_y))
+                return carry
+            lax.fori_loop(first, count_y, step, 0, unroll=few)
+
+        along_y(gz, 1)
+
+        def step_z(shift, carry):
+            along_y(lax.rem(gz + shift, count_z), 0)
+            return carry
+        lax.fori_loop(1, count_z, step_z, 0, unroll=few)
+
+    def greet(to_z, to_y):
+        pl.semaphore_signal(barrier, inc=1, device_id=(to_z, to_y), device_id_type=MESH)
+
+    each_other(greet)
+
+    loads[0].wait()
     owner = owners[...]
     before = hot(iota((chunk, chunk), 0) < iota((chunk, chunk), 1))
 
@@ -96,66 +111,48 @@
     ranks = over(groups, rank_group, jnp.zeros((1, rows), F32))
     rank_s[...] = hot(iota((LANES, rows), 0) == ranks.astype(jnp.int32))
 
-    load.wait()
+    loads[1].wait()
     row_s[...] = grid_v[:, 0, :]
     corner_s[...] = grid_v[0, 0:1, :]
     mesh_s[...] = with_diff(grid_v[...].reshape(slab, size_x))
 
-    pl.semaphore_wait(barrier, devices - 1)
-    below_z = lax.rem(gz + count_z - 1, count_z)
-    below_y = lax.rem(gy + count_y - 1, count_y)
-    halos = []
-    for i, (source, target, device) in enumerate((
-        (grid_ref.at[0], halo_z, (below_z, gy)),
-        (row_s, halo_y, (gz, below_y)),
-        (corner_s, halo_c, (below_z, below_y)),
-    )):
-        halos.append(pltpu.make_async_remote_copy(
-            src_ref=source, dst_ref=target, send_sem=halo_send.at[i], recv_sem=halo_recv.at[i],
-            device_id=device, device_id_type=MESH,
-        ))
-        halos[-1].start()
+    for copy in loads[2:]:
+        copy.wait()
 
     def place(j):
-        span = pl.ds(pl.multiple_of(j * chunk, chunk), chunk)
+        span = pl.ds(j * chunk, chunk)
         cell = cells[:, span]
         frac = (offsets[:, span].astype(F32) + 0.5) / 1024.0
         return (span, cell[0:1] - gz * size_z, cell[1:2] - gy * size_y, cell[2:3],
                 frac[0:1], frac[1:2], frac[2:3])
 
-    def main_chunk(j, carry):
+    def main_chunk(j):
         span, cz, cy, cx, fz, fy, fx = place(j)
         onehot = hot(iota((size_x, chunk), 0) == cx)
         hot_s[:, span] = onehot
         prod = dot_nn(mesh_s[...], onehot)
-        shape = (size_y, chunk)
-        cz, fz = jnp.broadcast_to(cz, shape), jnp.broadcast_to(fz, shape)
+        cz, fz = jnp.broadcast_to(cz, (8, chunk)), jnp.broadcast_to(fz, (8, chunk))
         gz0 = 1.0 - fz
-        total = [jnp.zeros(shape, F32) for _ in range(4)]
+        tiles = size_y // 8
+        total = [[jnp.zeros((8, chunk), F32) for _ in range(tiles)] for _ in range(4)]
         for z in range(size_z):
             lower, upper = cz == z, cz == z - 1
             weight = jnp.where(lower, gz0, jnp.where(upper, fz, 0.0))
             diff = jnp.where(lower, -1.0, jnp.where(upper, 1.0, 0.0))
-            at = [prod[q * slab + z * size_y:q * slab + (z + 1) * size_y] for q in range(4)]
-            value, slope = at[0] + at[1], at[2] + at[3]
-            total[0] += weight * value
-            total[1] += diff * value
-            total[2] += weight * slope
-            total[3] += diff * slope
+            for t in range(tiles):
+                first = z * size_y + 8 * t
+                at = [prod[q * slab + first:q * slab + first + 8] for q in range(4)]
+                value, slope = at[0] + at[1], at[2] + at[3]
+                total[0][t] += weight * value
+                total[1][t] += diff * value
+                total[2][t] += weight * slope
+                total[3][t] += diff * slope
         for q in range(4):
-            acc_s[q, :, span] = total[q]
-        return carry
-
-    lax.fori_loop(0, chunks, main_chunk, 0)
-
-    for copy in halos:
-        copy.wait()
-    ghost = jnp.concatenate(
-        [halo_z[...], halo_y[...], jnp.broadcast_to(halo_c[...], (8, size_x))], axis=0)
-    ghost = with_diff(ghost)
+            acc_s[q, :, span] = jnp.concatenate(total[q], axis=0)
+
     part = size_y + size_z + 8
 
-    def halo_chunk(j, carry):
+    def halo_chunk(j, ghost):
         span, cz, cy, cx, fz, fy, fx = place(j)
         prod = dot_nn(ghost, hot_s[:, span])
         value = prod[:part] + prod[part:2 * part]
@@ -188,9 +185,33 @@
         record = (slots[:, span] + 1).astype(F32)
         vals_s[:, span] = jnp.concatenate(
             [grad_z + wy_top * h_d, grad_y + dy_top * h_w, grad_x + wy_top * h_x, record] * 2, axis=0)
-        return carry
-
-    lax.fori_loop(0, chunks, halo_chunk, 0)
+
+    early = chunks // 4
+    for j in range(early):
+        main_chunk(j)
+    pl.semaphore_wait(barrier, devices - 1)
+    below_z = lax.rem(gz + count_z - 1, count_z)
+    below_y = lax.rem(gy + count_y - 1, count_y)
+    halos = []
+    for i, (source, target, device) in enumerate((
+        (grid_ref.at[0], halo_z, (below_z, gy)),
+        (row_s, halo_y, (gz, below_y)),
+        (corner_s, halo_c, (below_z, below_y)),
+    )):
+        halos.append(pltpu.make_async_remote_copy(
+            src_ref=source, dst_ref=target, send_sem=halo_send.at[i], recv_sem=halo_recv.at[i],
+            device_id=device, device_id_type=MESH,
+        ))
+        halos[-1].start()
+
+    for j in range(early, chunks):
+        main_chunk(j)
+    for copy in halos:
+        copy.wait()
+    ghost = with_diff(jnp.concatenate(
+        [halo_z[...], halo_y[...], jnp.broadcast_to(halo_c[...], (8, size_x))], axis=0))
+    for j in range(chunks):
+        halo_chunk(j, ghost)
 
     def pack_group(g, carry):
         wide = 4 * group
@@ -210,15 +231,14 @@
             device_id=device, device_id_type=MESH,
         )
 
-    def post(shift, carry):
-        other = lax.rem(me + shift, devices)
-        exchange(send_s.at[other], recv_s.at[me], coords(shift)).start()
-        return carry
-
-    lax.fori_loop(1, devices, post, 0)
+    def post(to_z, to_y):
+        other = to_z * count_y + to_y
+        exchange(send_s.at[other], recv_s.at[me], (to_z, to_y)).start()
+
+    each_other(post)
     recv_s[me] = send_s[me]
     others = pl.ds(0, devices - 1)
-    exchange(send_s.at[others], recv_s.at[others], coords(1)).wait()
+    exchange(send_s.at[others], recv_s.at[others], (below_z, below_y)).wait()
 
     highs = rows // LANES
 
@@ -245,13 +265,17 @@
     rows = cells.shape[1]
     devices = lax.axis_size("gz") * lax.axis_size("gy")
     vmem = pl.BlockSpec(memory_space=pltpu.VMEM)
-    part = size_y + size_z + 8
+    hbm = pl.BlockSpec(memory_space=pltpu.HBM)
     return pl.pallas_call(
         kernel,
         out_shape=jax.ShapeDtypeStruct((3, rows), F32),
-        in_specs=[pl.BlockSpec(memory_space=pl.ANY), vmem, vmem, vmem, vmem],
+        in_specs=[hbm] * 5,
         out_specs=vmem,
         scratch_shapes=[
+            pltpu.VMEM((3, rows), jnp.int32),
+            pltpu.VMEM((3, rows), jnp.int32),
+            pltpu.VMEM((1, rows), jnp.int32),
+            pltpu.VMEM((1, rows), jnp.int32),
             pltpu.VMEM((size_z, size_y, size_x), F32),
             pltpu.VMEM((size_z, size_x), F32),
             pltpu.VMEM((1, size_x), F32),
@@ -265,13 +289,13 @@
             pltpu.VMEM((8, rows), F32),
             pltpu.VMEM((devices, 4, LANES), F32),
             pltpu.VMEM((devices, 4, LANES), F32),
-            pltpu.SemaphoreType.DMA,
+            pltpu.SemaphoreType.DMA((5,)),
             pltpu.SemaphoreType.DMA((3,)),
             pltpu.SemaphoreType.DMA((3,)),
             pltpu.SemaphoreType.DMA,
             pltpu.SemaphoreType.DMA,
         ],
-        compiler_params=pltpu.CompilerParams(collective_id=0, has_side_effects=True),
+        compiler_params=pltpu.CompilerParams(collective_id=0, has_side_effects=True, vmem_limit_bytes=60 * 1024 * 1024),
         name="cic",
     )(grid_grad, cells, offsets, owners.reshape(1, rows), slots.reshape(1, rows))
 

time: 21.8 us -> 19.7 us (0.904)
  Pallas kernels: 20.1 us -> 18.2 us
    pallas_call x1, Pallas kernels: 20.1 us -> 18.2 us  [body(): pl.pallas_call(kernel, out_shape=jax.ShapeDtypeStruct((3, rows), F32), in...]
where the time goes in v2:
time: 19.7 us; the launch traced here: 19.6 us
  Pallas kernels  18.2 us (92%)
  local copies, waits for them, and re-layouts  1.38 us (7%)
    pallas_call x1, Pallas kernels, body(): pl.pallas_call(kernel, out_shape=jax.ShapeDtypeStruct((3, rows), F32), in...  18.2 us
    unnamed x1, local copies, waits for them, and re-layouts  1.38 us

profile of v2, /device:TPU:0, one launch (start us, length us, event | category | flops | bytes accessed | tf_op | source)
XLA Modules:
  0.0 19.6 jit_solution(18276618304983497492)
XLA Ops:
  0.0 18.2 %cic.1 = f32[3,2048]{1,0:T(4,128)} custom-call(f32[16,16,512]{2,1,0:T(8,128)} %grid_ref.1, s32[3,2048]{1,0:T(4,128)} %cells_ref.1, s32[3,2048]{1,0:T(4,128)} %offsets_ref.1, s32[1,2048]{1,0:T(1,128)} %bitcast.2, s32[1,2048]{1,0:T(1,128)} %bitcast.3), custom_call_target="tpu_custom_call" | custom-call | tf_op jit(solution)/shard_map/cic/pallas_call | solution.py:269
  18.2 1.4 %copy.7 = f32[3,2048]{1,0:T(4,128)} copy(f32[3,2048]{1,0:T(4,128)} %cic.1) | data formatting | bytes 49152

commit v3 on v2

--- a/solution.py
+++ b/solution.py
@@ -46,9 +46,9 @@
 
 
 def kernel(
-    grid_ref, cells_ref, offsets_ref, owners_ref, slots_ref, out,
+    grid_ref, cells_ref, offsets_ref, owners_ref, slots_ref, recv_s,
     cells, offsets, owners, slots, grid_v, row_s, corner_s, halo_z, halo_y, halo_c, mesh_s, hot_s, acc_s, rank_s, vals_s,
-    send_s, recv_s, load_sem, halo_send, halo_recv, all_send, all_recv,
+    send_s, load_sem, own_sem, halo_send, halo_recv, all_send, all_recv,
 ):
     count_z, count_y = lax.axis_size("gz"), lax.axis_size("gy")
     devices = count_z * count_y
@@ -80,12 +80,11 @@
                 return carry
             lax.fori_loop(first, count_y, step, 0, unroll=few)
 
-        along_y(gz, 1)
-
         def step_z(shift, carry):
             along_y(lax.rem(gz + shift, count_z), 0)
             return carry
         lax.fori_loop(1, count_z, step_z, 0, unroll=few)
+        along_y(gz, 1)
 
     def greet(to_z, to_y):
         pl.semaphore_signal(barrier, inc=1, device_id=(to_z, to_y), device_id_type=MESH)
@@ -194,9 +193,9 @@
     below_y = lax.rem(gy + count_y - 1, count_y)
     halos = []
     for i, (source, target, device) in enumerate((
+        (corner_s, halo_c, (below_z, below_y)),
         (grid_ref.at[0], halo_z, (below_z, gy)),
         (row_s, halo_y, (gz, below_y)),
-        (corner_s, halo_c, (below_z, below_y)),
     )):
         halos.append(pltpu.make_async_remote_copy(
             src_ref=source, dst_ref=target, send_sem=halo_send.at[i], recv_sem=halo_recv.at[i],
@@ -231,15 +230,23 @@
             device_id=device, device_id_type=MESH,
         )
 
+    own = pltpu.make_async_copy(send_s.at[me], recv_s.at[me], own_sem)
+
     def post(to_z, to_y):
         other = to_z * count_y + to_y
         exchange(send_s.at[other], recv_s.at[me], (to_z, to_y)).start()
 
     each_other(post)
-    recv_s[me] = send_s[me]
+    own.start()
+    own.wait()
     others = pl.ds(0, devices - 1)
     exchange(send_s.at[others], recv_s.at[others], (below_z, below_y)).wait()
 
+
+def scatter(recv_s, out):
+    devices, rows = recv_s.shape[0], out.shape[1]
+    group = min(32, devices)
+    groups = devices // group
     highs = rows // LANES
 
     def add_group(g, total):
@@ -266,11 +273,11 @@
     devices = lax.axis_size("gz") * lax.axis_size("gy")
     vmem = pl.BlockSpec(memory_space=pltpu.VMEM)
     hbm = pl.BlockSpec(memory_space=pltpu.HBM)
-    return pl.pallas_call(
+    received = pl.pallas_call(
         kernel,
-        out_shape=jax.ShapeDtypeStruct((3, rows), F32),
+        out_shape=jax.ShapeDtypeStruct((devices, 4, LANES), F32),
         in_specs=[hbm] * 5,
-        out_specs=vmem,
+        out_specs=hbm,
         scratch_shapes=[
             pltpu.VMEM((3, rows), jnp.int32),
             pltpu.VMEM((3, rows), jnp.int32),
@@ -288,8 +295,8 @@
             pltpu.VMEM((LANES, rows), BF),
             pltpu.VMEM((8, rows), F32),
             pltpu.VMEM((devices, 4, LANES), F32),
-            pltpu.VMEM((devices, 4, LANES), F32),
             pltpu.SemaphoreType.DMA((5,)),
+            pltpu.SemaphoreType.DMA,
             pltpu.SemaphoreType.DMA((3,)),
             pltpu.SemaphoreType.DMA((3,)),
             pltpu.SemaphoreType.DMA,
@@ -298,6 +305,14 @@
         compiler_params=pltpu.CompilerParams(collective_id=0, has_side_effects=True, vmem_limit_bytes=60 * 1024 * 1024),
         name="cic",
     )(grid_grad, cells, offsets, owners.reshape(1, rows), slots.reshape(1, rows))
+    return pl.pallas_call(
+        scatter,
+        out_shape=jax.ShapeDtypeStruct((3, rows), F32),
+        in_specs=[vmem],
+        out_specs=vmem,
+        compiler_params=pltpu.CompilerParams(vmem_limit_bytes=60 * 1024 * 1024),
+        name="scatter",
+    )(received)
 
 
 def solution(mesh):

time: 19.7 us -> 18.7 us (0.949)
  local copies, waits for them, and re-layouts: 1.38 us -> 0 us
  Pallas kernels: 18.2 us -> 18.5 us
    unnamed x1 -> x0, local copies, waits for them, and re-layouts: 1.38 us -> none
    pallas_call x1 -> x2, Pallas kernels: 18.2 us -> 18.5 us  [the longest x1 16.4 us: body(): pl.pallas_call(kernel, out_shape=jax.ShapeDtypeStruct((devices, 4, LANES)...]
where the time goes in v3:
time: 18.7 us; the launch traced here: 18.5 us
  Pallas kernels  18.5 us (99%)
    pallas_call x1, Pallas kernels, body(): pl.pallas_call(kernel, out_shape=jax.ShapeDtypeStruct((devices, 4, LANES)...  16.4 us
    pallas_call x1, Pallas kernels, body(): pl.pallas_call(scatter, out_shape=jax.ShapeDtypeStruct((3, rows), F32), i...  2.03 us

profile of v3, /device:TPU:0, one launch (start us, length us, event | category | flops | bytes accessed | tf_op | source)
XLA Modules:
  0.0 18.5 jit_solution(202153714551295690)
XLA Ops:
  0.0 16.4 %cic.1.recv_s = f32[32,4,128]{2,1,0:T(4,128)} custom-call(f32[16,16,512]{2,1,0:T(8,128)} %grid_ref.1, s32[3,2048]{1,0:T(4,128)} %cells_ref.1, s32[3,2048]{1,0:T(4,128)} %offsets_ref.1, s32[1,2048]{1,0:T(1,128)} %bitcast.2, s32[1,2048]{1,0:T(1,128)} %bitcast.3), custom_call_target="tpu_custom_call" | custom-call | tf_op jit(solution)/shard_map/cic/pallas_call | solution.py:276
  16.4 2.0 %scatter.1 = f32[3,2048]{1,0:T(4,128)} custom-call(f32[32,4,128]{2,1,0:T(4,128)} %cic.1.recv_s), custom_call_target="tpu_custom_call" | custom-call | tf_op jit(solution)/shard_map/scatter/pallas_call | solution.py:308
